TPU v7x, 128 devices: a whole 4x4x4 slice. The times are simulated.
128 devices in a mesh: grp: 2 (over x_lo), dev: 64 (over x_hi, z, y, core).
Axes of the slice: x: 4 (x_hi: 2, x_lo: 2; x = x_hi * 2 + x_lo), y: 4, z: 4, core: 2. Of those that a mesh axis runs over, the one named last changes fastest.
Arguments:
- frames: float32 [2, 128, 512, 512], P('grp', 'dev'), may hold values from -6 to 6
- ref_spectrum: float32 [2, 128, 512, 512], P(None, None, 'dev'), as said below
- shifts: int32 [2, 3], replicated, may hold values from 0 to 127
- offsets: int32 [2, 3], replicated, may hold values from 0 to 127
Outputs:
- correlation: float32 [2, 128, 128, 128], P('grp', 'dev')
- new_reference: float32 [2, 128, 512, 512], P(None, 'grp', 'dev')
Inputs may be any that keep to these rules, and one draw needn't show every extreme that they name: `ref_spectrum`: real and imaginary parts are real numbers.
All inputs are finite; a program needn't handle non-finite values.
Results may differ from a plain program's by a relative error of at most 0.0001.
Values sent between devices are 32-bit elements; how exact they have to be, the bound alone decides.
A program may use at most 128 MiB of HBM per device.

v0:
```python
import math

import jax
import jax.numpy as jnp
import numpy as np
from jax import lax
from jax.experimental import pallas as pl
from jax.experimental.pallas import tpu as pltpu
from jax.sharding import PartitionSpec as P

NX = 512
NY = 512
NZ = 128
CROP = 128
ROWS = 4
LANES = 128
BLOCKS = NX // LANES
WIDE = ROWS * LANES
DEVICES = 128
CHUNKS = 4
GROUPS = 16
SPAN = (GROUPS + 2) * 8
FACTOR = 1.0 / math.sqrt(NZ * NY * NX)
F32 = jnp.float32
BF16 = jnp.bfloat16
MESH = pl.DeviceIdType.MESH


def halves(table):
    single = table.astype(np.float32)
    high = single.astype(jnp.bfloat16)
    low = (table - high.astype(np.float64)).astype(np.float32).astype(jnp.bfloat16)
    return np.stack([high, low])


def forward_y_table():
    out = np.zeros((CHUNKS, GROUPS + 2, 2, ROWS, NY))
    y = np.arange(NY)
    for chunk in range(CHUNKS):
        for slot in range(GROUPS + 2):
            for j in range(ROWS):
                ky = 4 * (GROUPS * chunk + slot) + j
                angle = 2.0 * np.pi * (ky * y % NY) / NY
                out[chunk, slot, 0, j] = np.cos(angle)
                out[chunk, slot, 1, j] = -np.sin(angle)
    return halves(out.reshape(CHUNKS * SPAN, NY))


def forward_x_table():
    angle = 2.0 * np.pi * (np.arange(NX)[:, None] * np.arange(NX)[None, :] % NX) / NX
    return halves(np.concatenate([np.cos(angle), np.sin(angle)], axis=1))


def z_table(inverse):
    angle = 2.0 * np.pi * (np.arange(NZ)[:, None] * np.arange(NZ)[None, :] % NZ) / NZ
    c, s = np.cos(angle), np.sin(angle)
    if inverse:
        return halves(np.block([[c, -s], [s, c]]))
    return halves(FACTOR * np.block([[c, s], [-s, c]]))


def inverse_x_table():
    kx, x = np.arange(NX), np.arange(CROP)
    angle = 2.0 * np.pi * (kx[:, None] * x[None, :] % NX) / NX
    c, s = np.cos(angle), np.sin(angle)
    real = np.concatenate([c, s], axis=1).reshape(BLOCKS, LANES, 2 * CROP)
    imag = np.concatenate([-s, c], axis=1).reshape(BLOCKS, LANES, 2 * CROP)
    return halves(np.stack([real, imag], axis=1).reshape(2 * NX, 2 * CROP))


def inverse_y_table():
    group = np.arange(DEVICES)[:, None]
    j = np.arange(ROWS)[None, :]
    ky = 4 * group + np.where(group < DEVICES // 2, j, (4 - j) % 4)
    angle = 2.0 * np.pi * (np.arange(CROP)[:, None, None] * ky[None] % NY) / NY
    table = np.stack([np.cos(angle), -np.sin(angle)], axis=2)
    return halves(FACTOR * table.reshape(CROP, DEVICES * 8))


def split(a):
    high = a.astype(BF16)
    return high, (a - high.astype(F32)).astype(BF16)


def dot(a, b):
    return jnp.dot(a, b, preferred_element_type=F32)


def kernel(
    frames, dy, cs, zf, zi, xi, yi, shifts, offsets, ref_hbm,
    corr, nout,
    fhi, flo, sbuf, xbuf, rin, rbuf, cbuf, mbuf, nbuf, nrecv, ramp_xy, ramp_z,
    mine, abuf, g1hi, g1lo, gbuf, ybuf,
    send_x, recv_x, send_a, recv_a, send_n, recv_n, send_g, recv_g, ref_sem, own_sem,
):
    g = lax.axis_index("grp")
    d = lax.axis_index("dev")
    me = 2 * d + g
    core, y_at, z_at = d % 2, (d // 2) % 4, (d // 8) % 4
    upper = d // 32

    barrier = pltpu.get_barrier_semaphore()

    def greet(k, carry):
        to = (me + k) % DEVICES
        pl.semaphore_signal(barrier, 1, device_id=(to % 2, to // 2), device_id_type=MESH)
        return carry

    lax.fori_loop(1, DEVICES, greet, 0)
    for b in range(BLOCKS):
        pltpu.make_async_copy(ref_hbm.at[:, :, b * LANES : (b + 1) * LANES], rin.at[b], ref_sem).start()

    for p in range(2):
        high, low = split(frames[p])
        fhi[p] = high
        flo[p] = low

    sub = lax.broadcasted_iota(jnp.int32, (1, 8, NX), 1)
    sigma = jnp.where(sub < 4, 1.0, -1.0).astype(F32)
    first = (sub % 4) == 0

    def forward(i, carry):
        chunk = (z_at + i) % CHUNKS
        base = pl.multiple_of(chunk * SPAN, 16)
        dyh = dy[0, pl.ds(base, SPAN), :]
        dyl = dy[1, pl.ds(base, SPAN), :]
        for p in range(2):
            rows = dot(dyh, fhi[p]) + dot(dyh, flo[p]) + dot(dyl, fhi[p])
            rh, rl = split(rows)
            prod = dot(rh, cs[0]) + dot(rl, cs[0]) + dot(rh, cs[1])
            prod = prod.reshape(GROUPS + 2, 8, 2 * NX)
            m1 = prod[:, :, :NX]
            t1 = sigma * pltpu.roll(prod[:, :, NX:], 4, 1)
            plus = (m1 + t1)[:GROUPS]
            minus = sigma * (m1 - t1)
            minus = jnp.where(first, minus[1 : GROUPS + 1], minus[:GROUPS])
            for b in range(BLOCKS):
                lanes = slice(b * LANES, (b + 1) * LANES)
                sbuf[pl.ds(GROUPS * chunk, GROUPS), b, p * 8 : p * 8 + 8, :] = plus[:, :, lanes]
                sbuf[pl.ds(64 + GROUPS * chunk, GROUPS), b, p * 8 : p * 8 + 8, :] = minus[:, :, lanes]

        @pl.when(i == 0)
        def _():
            pl.semaphore_wait(barrier, DEVICES - 1)

        def send(k, inner):
            half = k % 2
            a, e, o = (k // 2) % 4, (k // 8) % 2, k // 16
            within = 4 * ((y_at + a) % 4) + 2 * ((core + o) % 2) + (g + e) % 2
            to = jnp.where(half == 0, GROUPS * chunk + within, 64 + GROUPS * (3 - chunk) + within)
            slot = jnp.where(half == 0, GROUPS * chunk + within, 64 + GROUPS * chunk + 15 - within)

            @pl.when(to != me)
            def _():
                pltpu.make_async_remote_copy(
                    sbuf.at[slot], xbuf.at[g, :, pl.ds(16 * d, 16)], send_x, recv_x,
                    device_id=(to % 2, to // 2), device_id_type=MESH,
                ).start()

            @pl.when(to == me)
            def _():
                pltpu.make_async_copy(sbuf.at[slot], xbuf.at[g, :, pl.ds(16 * d, 16)], own_sem).start()

            return inner

        lax.fori_loop(0, 32, send, 0)
        return carry

    lax.fori_loop(0, CHUNKS, forward, 0)

    def row_of(j):
        return jnp.where(upper == 0, j, (4 - j) % 4)

    pltpu.make_async_copy(rin, rin, ref_sem).wait()
    for part in range(2):
        for j in range(ROWS):
            for b in range(BLOCKS):
                rbuf[part, b, :, j * LANES : (j + 1) * LANES] = rin[
                    b, part, pl.ds(4 * g + row_of(j), NZ, stride=8), :
                ]

    lane = lax.broadcasted_iota(jnp.int32, (8, WIDE), 1)
    j_of = lane // LANES
    ky = 8 * d + 4 * g + jnp.where(upper == 0, j_of, (4 - j_of) % 4)
    kz = lax.broadcasted_iota(jnp.int32, (NZ, LANES), 0)
    unit = 2.0 * math.pi / NX
    for which, source in enumerate((shifts, offsets)):
        for t in range(2):
            sign = -1.0 if which == 0 else 1.0
            phase = (kz * source[t, 0]) % NZ
            angle = (4.0 * unit) * phase.astype(F32)
            ramp_z[which, t, 0] = jnp.cos(angle)
            ramp_z[which, t, 1] = sign * jnp.sin(angle)
            for b in range(BLOCKS):
                kx = b * LANES + lane % LANES
                phase = (ky * source[t, 1] + kx * source[t, 2]) % NX
                angle = unit * phase.astype(F32)
                ramp_xy[which, t, b, 0] = jnp.cos(angle)
                ramp_xy[which, t, b, 1] = sign * jnp.sin(angle)

    def turned(which, t, b, re, im):
        zr, zs = ramp_z[which, t, 0], ramp_z[which, t, 1]
        xr = ramp_xy[which, t, b, 0][:1]
        xs = ramp_xy[which, t, b, 1][:1]
        out_re, out_im = [], []
        for j in range(ROWS):
            lanes = slice(j * LANES, (j + 1) * LANES)
            ar, ai = xr[:, lanes], xs[:, lanes]
            cr = zr * ar - zs * ai
            ci = zr * ai + zs * ar
            out_re.append(re[:, lanes] * cr - im[:, lanes] * ci)
            out_im.append(re[:, lanes] * ci + im[:, lanes] * cr)
        return jnp.concatenate(out_re, axis=1), jnp.concatenate(out_im, axis=1)

    pltpu.make_async_copy(sbuf.at[0], sbuf.at[0], own_sem).wait()
    pltpu.make_async_copy(sbuf.at[pl.ds(0, DEVICES - 1)], sbuf.at[pl.ds(0, DEVICES - 1)], recv_x).wait()

    def spectrum(b, sums):
        zh, zl = zf[0], zf[1]
        ref_re, ref_im = rbuf[0, b], rbuf[1, b]
        new_re, new_im = 0.5 * ref_re, 0.5 * ref_im
        found = []
        for t in range(2):
            re = [xbuf[t, b, pl.ds(j, NZ, stride=8), :] for j in range(ROWS)]
            im = [xbuf[t, b, pl.ds(4 + j, NZ, stride=8), :] for j in range(ROWS)]
            both = jnp.concatenate([jnp.concatenate(re, axis=1), jnp.concatenate(im, axis=1)], axis=0)
            bh, bl = split(both)
            freq = dot(zh, bh) + dot(zl, bh) + dot(zh, bl)
            fr, fi = freq[:NZ], freq[NZ:]
            cross_re = fr * ref_re + fi * ref_im
            cross_im = fi * ref_re - fr * ref_im
            magnitude = jnp.sqrt(cross_re * cross_re + cross_im * cross_im)
            cbuf[t, b, :NZ] = cross_re
            cbuf[t, b, NZ:] = cross_im
            mbuf[t, b] = magnitude
            found.append(sums[t] + magnitude.reshape(NZ // 8, 8, WIDE).sum(axis=0))
            wr, wi = turned(0, t, b, fr, fi)
            new_re += 0.25 * wr
            new_im += 0.25 * wi
        nbuf[b, 0] = new_re
        nbuf[b, 1] = new_im
        return tuple(found)

    sums = lax.fori_loop(0, BLOCKS, spectrum, (jnp.zeros((8, WIDE), F32),) * 2)

    lane1 = lax.broadcasted_iota(jnp.int32, (1, LANES), 1)
    mine[...] = jnp.where(lane1 < 64, jnp.sum(sums[0]), jnp.sum(sums[1]))

    def tell(k, carry):
        to = (me + k) % DEVICES
        pltpu.make_async_remote_copy(
            mine, abuf.at[me], send_a, recv_a, device_id=(to % 2, to // 2), device_id_type=MESH
        ).start()
        return carry

    lax.fori_loop(1, DEVICES, tell, 0)
    pltpu.make_async_copy(mine, abuf.at[me], own_sem).start()

    half = NZ // 2
    partner_copy = pltpu.make_async_remote_copy(
        nbuf.at[:, :, pl.ds((1 - g) * half, half)], nrecv, send_n, recv_n,
        device_id=(1 - g, d), device_id_type=MESH,
    )
    partner_copy.start()

    def keep(source, at_grp):
        for b in range(BLOCKS):
            for part in range(2):
                for j in range(ROWS):
                    nout[part, b, pl.ds(4 * at_grp + row_of(j), half, stride=8), :] = source[
                        b, part, :, j * LANES : (j + 1) * LANES
                    ]

    keep(nbuf.at[:, :, pl.ds(g * half, half)], g)

    pltpu.make_async_copy(mine, abuf.at[me], own_sem).wait()
    pltpu.make_async_copy(abuf.at[pl.ds(0, DEVICES - 1)], abuf.at[pl.ds(0, DEVICES - 1)], recv_a).wait()
    total = jnp.sum(abuf[...].reshape(DEVICES, LANES), axis=0, keepdims=True) / (NZ * NY * NX)

    def back(i, carry):
        t = (g + i) % 2
        average = jnp.sum(jnp.where(lane1 == 64 * t, total, 0.0))

        def whiten(b, inner):
            zh, zl = zi[0], zi[1]
            scale = 1.0 / (mbuf[t, b] + average)
            wr, wi = turned(1, t, b, cbuf[t, b, :NZ] * scale, cbuf[t, b, NZ:] * scale)
            both = jnp.concatenate([wr, wi], axis=0)
            bh, bl = split(both)
            depth = dot(zh, bh) + dot(zl, bh) + dot(zh, bl)
            dh, dl = split(depth)
            for part in range(2):
                for j in range(ROWS):
                    at = pl.ds(pl.multiple_of((2 * b + part) * LANES, LANES), LANES)
                    rows = slice(part * NZ, (part + 1) * NZ)
                    lanes = slice(j * LANES, (j + 1) * LANES)
                    g1hi[j * NZ : (j + 1) * NZ, at] = dh[rows, lanes]
                    g1lo[j * NZ : (j + 1) * NZ, at] = dl[rows, lanes]
            return inner

        lax.fori_loop(0, BLOCKS, whiten, 0)
        width = dot(g1hi[...], xi[0]) + dot(g1lo[...], xi[0]) + dot(g1hi[...], xi[1])
        for part in range(2):
            for j in range(ROWS):
                gbuf[t, pl.ds(4 * part + j, NZ, stride=8), :] = width[
                    j * NZ : (j + 1) * NZ, part * CROP : (part + 1) * CROP
                ]

        def send(k, inner):
            to = (d + k) % 64

            @pl.when((to != d) | (t != g))
            def _():
                pltpu.make_async_remote_copy(
                    gbuf.at[t, pl.ds(16 * to, 16)], ybuf.at[me], send_g, recv_g,
                    device_id=(t, to), device_id_type=MESH,
                ).start()

            @pl.when((to == d) & (t == g))
            def _():
                pltpu.make_async_copy(gbuf.at[t, pl.ds(16 * to, 16)], ybuf.at[me], own_sem).start()

            return inner

        lax.fori_loop(0, 64, send, 0)
        return carry

    lax.fori_loop(0, 2, back, 0)

    pltpu.make_async_copy(ybuf.at[0], ybuf.at[0], own_sem).wait()
    pltpu.make_async_copy(ybuf.at[pl.ds(0, DEVICES - 1)], ybuf.at[pl.ds(0, DEVICES - 1)], recv_g).wait()
    for p in range(2):
        rows = ybuf[:, p * 8 : p * 8 + 8, :].reshape(DEVICES * 8, CROP)
        rh, rl = split(rows)
        corr[p] = dot(yi[0], rh) + dot(yi[1], rh) + dot(yi[0], rl)

    partner_copy.wait_recv()
    keep(nrecv, 1 - g)

    pltpu.make_async_copy(sbuf.at[pl.ds(0, DEVICES - 1)], sbuf.at[pl.ds(0, DEVICES - 1)], send_x).wait()
    pltpu.make_async_copy(abuf.at[pl.ds(0, DEVICES - 1)], abuf.at[pl.ds(0, DEVICES - 1)], send_a).wait()
    pltpu.make_async_copy(ybuf.at[pl.ds(0, DEVICES - 1)], ybuf.at[pl.ds(0, DEVICES - 1)], send_g).wait()
    partner_copy.wait_send()


def local(frames, ref_spectrum, shifts, offsets):
    vmem = pl.BlockSpec(memory_space=pltpu.VMEM)
    smem = pl.BlockSpec(memory_space=pltpu.SMEM)
    corr, new = pl.pallas_call(
        kernel,
        out_shape=(
            jax.ShapeDtypeStruct((2, CROP, CROP), F32),
            jax.ShapeDtypeStruct((2, BLOCKS, NZ // 2 * 8, LANES), F32),
        ),
        in_specs=[vmem] * 7 + [smem] * 2 + [pl.BlockSpec(memory_space=pl.ANY)],
        out_specs=(vmem, vmem),
        scratch_shapes=[
            pltpu.VMEM((2, NY, NX), BF16),
            pltpu.VMEM((2, NY, NX), BF16),
            pltpu.VMEM((DEVICES, BLOCKS, 16, LANES), F32),
            pltpu.VMEM((2, BLOCKS, NZ * 8, LANES), F32),
            pltpu.VMEM((BLOCKS, 2, NZ * 8, LANES), F32),
            pltpu.VMEM((2, BLOCKS, NZ, WIDE), F32),
            pltpu.VMEM((2, BLOCKS, 2 * NZ, WIDE), F32),
            pltpu.VMEM((2, BLOCKS, NZ, WIDE), F32),
            pltpu.VMEM((BLOCKS, 2, NZ, WIDE), F32),
            pltpu.VMEM((BLOCKS, 2, NZ // 2, WIDE), F32),
            pltpu.VMEM((2, 2, BLOCKS, 2, 8, WIDE), F32),
            pltpu.VMEM((2, 2, 2, NZ, LANES), F32),
            pltpu.VMEM((1, LANES), F32),
            pltpu.VMEM((DEVICES, 1, LANES), F32),
            pltpu.VMEM((ROWS * NZ, 2 * NX), BF16),
            pltpu.VMEM((ROWS * NZ, 2 * NX), BF16),
            pltpu.VMEM((2, NZ * 8, LANES), F32),
            pltpu.VMEM((DEVICES, 16, LANES), F32),
        ]
        + [pltpu.SemaphoreType.DMA] * 10,
        compiler_params=pltpu.CompilerParams(
            collective_id=0, has_side_effects=True, vmem_limit_bytes=60 << 20
        ),
    )(
        frames[0],
        jnp.asarray(forward_y_table()),
        jnp.asarray(forward_x_table()),
        jnp.asarray(z_table(False)),
        jnp.asarray(z_table(True)),
        jnp.asarray(inverse_x_table()),
        jnp.asarray(inverse_y_table()),
        shifts,
        offsets,
        ref_spectrum.reshape(2, NZ * 8, NX),
    )
    new = new.reshape(2, BLOCKS, NZ // 2, 8, LANES).transpose(0, 2, 3, 1, 4)
    return corr[None], new.reshape(2, NZ // 2, 8, NX)


def solution(mesh):
    return jax.shard_map(
        local,
        mesh=mesh,
        in_specs=(P("grp", "dev", None, None), P(None, None, "dev", None), P(), P()),
        out_specs=(P("grp", "dev", None, None), P(None, "grp", "dev", None)),
        check_vma=False,
    )
```

profile of v0, /device:TPU:5, one launch (start us, length us, event | category | flops | bytes accessed | tf_op | source)
XLA Modules:
  0.0 136.3 jit_solution(4389509085504226932)
XLA Ops:
  0.6 131.8 %shard_map.113 = (f32[2,128,128]{2,1,0:T(8,128)}, f32[2,4,512,128]{3,2,1,0:T(8,128)}) custom-call(f32[2,512,512]{2,1,0:T(8,128)} %bitcast.11, bf16[2,576,512]{2,1,0:T(8,128)(2,1)} %constant.12.clone.dy, bf16[2,512,1024]{2,1,0:T(8,128)(2,1)} %constant.13.clone.cs, bf16[2,256,256]{2,1,0:T(8,128)(2,1)} %constant.14.clone.zf, ...), custom_call_target="tpu_custom_call" | custom-call | tf_op jit(solution)/shard_map/pallas_call | solution.py:349
  132.4 0.0 copy-start
  132.4 3.2 %copy_bitcast_fusion = f32[2,64,8,512]{3,2,1,0:T(8,128)} fusion(f32[2,4,512,128]{3,2,1,0:T(8,128)} %get-tuple-element.5), kind=kLoop, calls=%fused_computation | loop fusion | bytes 4194304 | tf_op jit(solution)/shard_map/reshape | solution.py:394
  135.7 0.0 copy-done
  135.7 0.7 copy.15
Async XLA Ops:
  132.4 3.3 %copy-start = (f32[2,128,128]{2,1,0:T(8,128)S(1)}, f32[2,128,128]{2,1,0:T(8,128)}, u32[]{:S(2)}) copy-start(f32[2,128,128]{2,1,0:T(8,128)} %get-tuple-element.4) | copy-start | bytes 393220
where the time goes:
time: 136 us
  Pallas kernels  132 us (97%)
  local copies, waits for them, and re-layouts  3.9 us (3%)
    pallas_call x1, Pallas kernels, local(): pl.pallas_call(kernel, out_shape=(jax.ShapeDtypeStruct((2, CROP, CROP), F...  132 us
    reshape x1, local copies, waits for them, and re-layouts, local(): return (corr[None], new.reshape(2, NZ // 2, 8, NX))  3.24 us

commit v1 on v0

--- a/solution.py
+++ b/solution.py
@@ -19,7 +19,7 @@
 DEVICES = 128
 CHUNKS = 4
 GROUPS = 16
-SPAN = (GROUPS + 2) * 8
+SPAN = (GROUPS + 4) * 8
 FACTOR = 1.0 / math.sqrt(NZ * NY * NX)
 F32 = jnp.float32
 BF16 = jnp.bfloat16
@@ -34,15 +34,16 @@
 
 
 def forward_y_table():
-    out = np.zeros((CHUNKS, GROUPS + 2, 2, ROWS, NY))
+    out = np.zeros((CHUNKS, 4, 5, 2, ROWS, NY))
     y = np.arange(NY)
     for chunk in range(CHUNKS):
-        for slot in range(GROUPS + 2):
-            for j in range(ROWS):
-                ky = 4 * (GROUPS * chunk + slot) + j
-                angle = 2.0 * np.pi * (ky * y % NY) / NY
-                out[chunk, slot, 0, j] = np.cos(angle)
-                out[chunk, slot, 1, j] = -np.sin(angle)
+        for run in range(4):
+            for at in range(5):
+                for j in range(ROWS):
+                    ky = 4 * (16 * run + 4 * ((chunk - run) % 4) + at) + j
+                    angle = 2.0 * np.pi * (ky * y % NY) / NY
+                    out[chunk, run, at, 0, j] = np.cos(angle)
+                    out[chunk, run, at, 1, j] = -np.sin(angle)
     return halves(out.reshape(CHUNKS * SPAN, NY))
 
 
@@ -120,7 +121,7 @@
     first = (sub % 4) == 0
 
     def forward(i, carry):
-        chunk = (z_at + i) % CHUNKS
+        chunk = (y_at + z_at + i) % CHUNKS
         base = pl.multiple_of(chunk * SPAN, 16)
         dyh = dy[0, pl.ds(base, SPAN), :]
         dyl = dy[1, pl.ds(base, SPAN), :]
@@ -128,12 +129,12 @@
             rows = dot(dyh, fhi[p]) + dot(dyh, flo[p]) + dot(dyl, fhi[p])
             rh, rl = split(rows)
             prod = dot(rh, cs[0]) + dot(rl, cs[0]) + dot(rh, cs[1])
-            prod = prod.reshape(GROUPS + 2, 8, 2 * NX)
+            prod = prod.reshape(GROUPS + 4, 8, 2 * NX)
             m1 = prod[:, :, :NX]
             t1 = sigma * pltpu.roll(prod[:, :, NX:], 4, 1)
-            plus = (m1 + t1)[:GROUPS]
-            minus = sigma * (m1 - t1)
-            minus = jnp.where(first, minus[1 : GROUPS + 1], minus[:GROUPS])
+            plus = (m1 + t1).reshape(4, 5, 8, NX)[:, :4].reshape(GROUPS, 8, NX)
+            minus = (sigma * (m1 - t1)).reshape(4, 5, 8, NX)
+            minus = jnp.where(first[None], minus[:, 1:], minus[:, :4]).reshape(GROUPS, 8, NX)
             for b in range(BLOCKS):
                 lanes = slice(b * LANES, (b + 1) * LANES)
                 sbuf[pl.ds(GROUPS * chunk, GROUPS), b, p * 8 : p * 8 + 8, :] = plus[:, :, lanes]
@@ -144,11 +145,12 @@
             pl.semaphore_wait(barrier, DEVICES - 1)
 
         def send(k, inner):
-            half = k % 2
-            a, e, o = (k // 2) % 4, (k // 8) % 2, k // 16
-            within = 4 * ((y_at + a) % 4) + 2 * ((core + o) % 2) + (g + e) % 2
-            to = jnp.where(half == 0, GROUPS * chunk + within, 64 + GROUPS * (3 - chunk) + within)
-            slot = jnp.where(half == 0, GROUPS * chunk + within, 64 + GROUPS * chunk + 15 - within)
+            half = (k + upper) % 2
+            to_z = (z_at + k // 2) % 4
+            to_y = jnp.where(half == 0, chunk + 8 - to_z, 10 - chunk - to_z) % 4
+            within = 2 * ((core + k // 16) % 2) + (g + k // 8) % 2
+            to = 64 * half + 16 * to_z + 4 * to_y + within
+            slot = jnp.where(half == 0, GROUPS * chunk + 4 * to_z + within, 79 + GROUPS * chunk - 4 * to_z - within)
 
             @pl.when(to != me)
             def _():
@@ -214,6 +216,14 @@
 
     pltpu.make_async_copy(sbuf.at[0], sbuf.at[0], own_sem).wait()
     pltpu.make_async_copy(sbuf.at[pl.ds(0, DEVICES - 1)], sbuf.at[pl.ds(0, DEVICES - 1)], recv_x).wait()
+
+    half = NZ // 2
+
+    def to_partner(b):
+        return pltpu.make_async_remote_copy(
+            nbuf.at[b, :, pl.ds((1 - g) * half, half)], nrecv.at[b], send_n, recv_n,
+            device_id=(1 - g, d), device_id_type=MESH,
+        )
 
     def spectrum(b, sums):
         zh, zl = zf[0], zf[1]
@@ -239,6 +249,11 @@
             new_im += 0.25 * wi
         nbuf[b, 0] = new_re
         nbuf[b, 1] = new_im
+
+        @pl.when(b == 0)
+        def _():
+            to_partner(b).start()
+
         return tuple(found)
 
     sums = lax.fori_loop(0, BLOCKS, spectrum, (jnp.zeros((8, WIDE), F32),) * 2)
@@ -256,12 +271,8 @@
     lax.fori_loop(1, DEVICES, tell, 0)
     pltpu.make_async_copy(mine, abuf.at[me], own_sem).start()
 
-    half = NZ // 2
-    partner_copy = pltpu.make_async_remote_copy(
-        nbuf.at[:, :, pl.ds((1 - g) * half, half)], nrecv, send_n, recv_n,
-        device_id=(1 - g, d), device_id_type=MESH,
-    )
-    partner_copy.start()
+    for b in range(1, BLOCKS):
+        to_partner(b).start()
 
     def keep(source, at_grp):
         for b in range(BLOCKS):
@@ -334,13 +345,13 @@
         rh, rl = split(rows)
         corr[p] = dot(yi[0], rh) + dot(yi[1], rh) + dot(yi[0], rl)
 
-    partner_copy.wait_recv()
+    pltpu.make_async_copy(nrecv, nrecv, recv_n).wait()
     keep(nrecv, 1 - g)
 
     pltpu.make_async_copy(sbuf.at[pl.ds(0, DEVICES - 1)], sbuf.at[pl.ds(0, DEVICES - 1)], send_x).wait()
     pltpu.make_async_copy(abuf.at[pl.ds(0, DEVICES - 1)], abuf.at[pl.ds(0, DEVICES - 1)], send_a).wait()
     pltpu.make_async_copy(ybuf.at[pl.ds(0, DEVICES - 1)], ybuf.at[pl.ds(0, DEVICES - 1)], send_g).wait()
-    partner_copy.wait_send()
+    pltpu.make_async_copy(nrecv, nrecv, send_n).wait()
 
 
 def local(frames, ref_spectrum, shifts, offsets):

time: 136 us -> 109 us (0.80)
  Pallas kernels: 132 us -> 104 us
    pallas_call x1, Pallas kernels: 132 us -> 104 us  [local(): pl.pallas_call(kernel, out_shape=(jax.ShapeDtypeStruct((2, CROP, CROP), F...]
where the time goes in v1:
time: 109 us; the launch traced here: 108 us
  Pallas kernels  104 us (95%)
  local copies, waits for them, and re-layouts  3.9 us (4%)
    pallas_call x1, Pallas kernels, local(): pl.pallas_call(kernel, out_shape=(jax.ShapeDtypeStruct((2, CROP, CROP), F...  104 us
    reshape x1, local copies, waits for them, and re-layouts, local(): return (corr[None], new.reshape(2, NZ // 2, 8, NX))  3.24 us

profile of v1, /device:TPU:5, one launch (start us, length us, event | category | flops | bytes accessed | tf_op | source)
XLA Modules:
  0.0 108.5 jit_solution(2154346348889560176)
XLA Ops:
  0.6 103.9 %shard_map.113 = (f32[2,128,128]{2,1,0:T(8,128)}, f32[2,4,512,128]{3,2,1,0:T(8,128)}) custom-call(f32[2,512,512]{2,1,0:T(8,128)} %bitcast.11, bf16[2,640,512]{2,1,0:T(8,128)(2,1)} %constant.12.clone.dy, bf16[2,512,1024]{2,1,0:T(8,128)(2,1)} %constant.13.clone.cs, bf16[2,256,256]{2,1,0:T(8,128)(2,1)} %constant.14.clone.zf, ...), custom_call_target="tpu_custom_call" | custom-call | tf_op jit(solution)/shard_map/pallas_call | solution.py:360
  104.6 0.0 copy-start
  104.6 3.2 %copy_bitcast_fusion = f32[2,64,8,512]{3,2,1,0:T(8,128)} fusion(f32[2,4,512,128]{3,2,1,0:T(8,128)} %get-tuple-element.5), kind=kLoop, calls=%fused_computation | loop fusion | bytes 4194304 | tf_op jit(solution)/shard_map/reshape | solution.py:405
  107.8 0.0 copy-done
  107.8 0.7 copy.15
Async XLA Ops:
  104.6 3.3 %copy-start = (f32[2,128,128]{2,1,0:T(8,128)S(1)}, f32[2,128,128]{2,1,0:T(8,128)}, u32[]{:S(2)}) copy-start(f32[2,128,128]{2,1,0:T(8,128)} %get-tuple-element.4) | copy-start | bytes 393220

commit v2 on v1

--- a/solution.py
+++ b/solution.py
@@ -88,11 +88,13 @@
 
 
 def kernel(
-    frames, dy, cs, zf, zi, xi, yi, shifts, offsets, ref_hbm,
+    frames_hbm, dy_hbm, cs_hbm, zf_hbm, zi_hbm, xi_hbm, yi_hbm, shifts_hbm, offsets_hbm, ref_hbm,
     corr, nout,
+    frames, dy, cs, zf, zi, xi, yi, shifts, offsets,
     fhi, flo, sbuf, xbuf, rin, rbuf, cbuf, mbuf, nbuf, nrecv, ramp_xy, ramp_z,
     mine, abuf, g1hi, g1lo, gbuf, ybuf,
     send_x, recv_x, send_a, recv_a, send_n, recv_n, send_g, recv_g, ref_sem, own_sem,
+    recv_y, first_sem, table_sem,
 ):
     g = lax.axis_index("grp")
     d = lax.axis_index("dev")
@@ -102,23 +104,60 @@
 
     barrier = pltpu.get_barrier_semaphore()
 
+    early = [(frames_hbm, frames), (dy_hbm, dy), (cs_hbm, cs)]
+    late = [(zf_hbm, zf), (zi_hbm, zi), (xi_hbm, xi), (yi_hbm, yi), (shifts_hbm, shifts), (offsets_hbm, offsets)]
+    early = [pltpu.make_async_copy(a, b, first_sem.at[i]) for i, (a, b) in enumerate(early)]
+    late = [pltpu.make_async_copy(a, b, table_sem.at[i]) for i, (a, b) in enumerate(late)]
+    for copy in early:
+        copy.start()
+
     def greet(k, carry):
-        to = (me + k) % DEVICES
+        to = (me + 104 + k + jnp.where(k >= 24, 1, 0)) % DEVICES
         pl.semaphore_signal(barrier, 1, device_id=(to % 2, to // 2), device_id_type=MESH)
         return carry
 
-    lax.fori_loop(1, DEVICES, greet, 0)
+    lax.fori_loop(0, DEVICES - 1, greet, 0)
+    for copy in late:
+        copy.start()
     for b in range(BLOCKS):
         pltpu.make_async_copy(ref_hbm.at[:, :, b * LANES : (b + 1) * LANES], rin.at[b], ref_sem).start()
 
+    early[0].wait()
     for p in range(2):
         high, low = split(frames[p])
         fhi[p] = high
         flo[p] = low
 
+    early[1].wait()
+    early[2].wait()
     sub = lax.broadcasted_iota(jnp.int32, (1, 8, NX), 1)
     sigma = jnp.where(sub < 4, 1.0, -1.0).astype(F32)
     first = (sub % 4) == 0
+
+    pair = BLOCKS // 2
+
+    def send(chunk, k, which):
+        half = (k + upper) % 2
+        to_z = (z_at + k // 2) % 4
+        to_y = jnp.where(half == 0, chunk + 8 - to_z, 10 - chunk - to_z) % 4
+        within = 2 * ((core + k // 16) % 2) + (g + k // 8) % 2
+        to = 64 * half + 16 * to_z + 4 * to_y + within
+        slot = jnp.where(half == 0, GROUPS * chunk + 4 * to_z + within, 79 + GROUPS * chunk - 4 * to_z - within)
+        blocks = slice(which * pair, (which + 1) * pair)
+        source, target = sbuf.at[slot, blocks], xbuf.at[g, blocks, pl.ds(16 * d, 16)]
+
+        @pl.when(to != me)
+        def _():
+            pltpu.make_async_remote_copy(
+                source, target, send_x, recv_y if which else recv_x,
+                device_id=(to % 2, to // 2), device_id_type=MESH,
+            ).start()
+
+        @pl.when(to == me)
+        def _():
+            pltpu.make_async_copy(source, target, own_sem).start()
+
+        return 0
 
     def forward(i, carry):
         chunk = (y_at + z_at + i) % CHUNKS
@@ -144,35 +183,17 @@
         def _():
             pl.semaphore_wait(barrier, DEVICES - 1)
 
-        def send(k, inner):
-            half = (k + upper) % 2
-            to_z = (z_at + k // 2) % 4
-            to_y = jnp.where(half == 0, chunk + 8 - to_z, 10 - chunk - to_z) % 4
-            within = 2 * ((core + k // 16) % 2) + (g + k // 8) % 2
-            to = 64 * half + 16 * to_z + 4 * to_y + within
-            slot = jnp.where(half == 0, GROUPS * chunk + 4 * to_z + within, 79 + GROUPS * chunk - 4 * to_z - within)
-
-            @pl.when(to != me)
-            def _():
-                pltpu.make_async_remote_copy(
-                    sbuf.at[slot], xbuf.at[g, :, pl.ds(16 * d, 16)], send_x, recv_x,
-                    device_id=(to % 2, to // 2), device_id_type=MESH,
-                ).start()
-
-            @pl.when(to == me)
-            def _():
-                pltpu.make_async_copy(sbuf.at[slot], xbuf.at[g, :, pl.ds(16 * d, 16)], own_sem).start()
-
-            return inner
-
-        lax.fori_loop(0, 32, send, 0)
+        lax.fori_loop(0, 32, lambda k, inner: send(chunk, k, 0), 0)
         return carry
 
     lax.fori_loop(0, CHUNKS, forward, 0)
+    lax.fori_loop(0, 32 * CHUNKS, lambda k, inner: send((y_at + z_at + k // 32) % CHUNKS, k % 32, 1), 0)
 
     def row_of(j):
         return jnp.where(upper == 0, j, (4 - j) % 4)
 
+    for copy in late:
+        copy.wait()
     pltpu.make_async_copy(rin, rin, ref_sem).wait()
     for part in range(2):
         for j in range(ROWS):
@@ -215,7 +236,8 @@
         return jnp.concatenate(out_re, axis=1), jnp.concatenate(out_im, axis=1)
 
     pltpu.make_async_copy(sbuf.at[0], sbuf.at[0], own_sem).wait()
-    pltpu.make_async_copy(sbuf.at[pl.ds(0, DEVICES - 1)], sbuf.at[pl.ds(0, DEVICES - 1)], recv_x).wait()
+    arrivals = sbuf.at[pl.ds(0, DEVICES - 1), 0:pair]
+    pltpu.make_async_copy(arrivals, arrivals, recv_x).wait()
 
     half = NZ // 2
 
@@ -226,6 +248,10 @@
         )
 
     def spectrum(b, sums):
+        @pl.when(b == pair)
+        def _():
+            pltpu.make_async_copy(arrivals, arrivals, recv_y).wait()
+
         zh, zl = zf[0], zf[1]
         ref_re, ref_im = rbuf[0, b], rbuf[1, b]
         new_re, new_im = 0.5 * ref_re, 0.5 * ref_im
@@ -278,7 +304,7 @@
         for b in range(BLOCKS):
             for part in range(2):
                 for j in range(ROWS):
-                    nout[part, b, pl.ds(4 * at_grp + row_of(j), half, stride=8), :] = source[
+                    nout[part, pl.ds(8 * b + 4 * at_grp + row_of(j), half, stride=8 * BLOCKS), :] = source[
                         b, part, :, j * LANES : (j + 1) * LANES
                     ]
 
@@ -356,16 +382,25 @@
 
 def local(frames, ref_spectrum, shifts, offsets):
     vmem = pl.BlockSpec(memory_space=pltpu.VMEM)
-    smem = pl.BlockSpec(memory_space=pltpu.SMEM)
+    hbm = pl.BlockSpec(memory_space=pltpu.HBM)
     corr, new = pl.pallas_call(
         kernel,
         out_shape=(
             jax.ShapeDtypeStruct((2, CROP, CROP), F32),
-            jax.ShapeDtypeStruct((2, BLOCKS, NZ // 2 * 8, LANES), F32),
+            jax.ShapeDtypeStruct((2, NZ // 2 * BLOCKS * 8, LANES), F32),
         ),
-        in_specs=[vmem] * 7 + [smem] * 2 + [pl.BlockSpec(memory_space=pl.ANY)],
+        in_specs=[hbm] * 10,
         out_specs=(vmem, vmem),
         scratch_shapes=[
+            pltpu.VMEM((2, NY, NX), F32),
+            pltpu.VMEM((2, CHUNKS * SPAN, NY), BF16),
+            pltpu.VMEM((2, NX, 2 * NX), BF16),
+            pltpu.VMEM((2, 2 * NZ, 2 * NZ), BF16),
+            pltpu.VMEM((2, 2 * NZ, 2 * NZ), BF16),
+            pltpu.VMEM((2, 2 * NX, 2 * CROP), BF16),
+            pltpu.VMEM((2, CROP, DEVICES * 8), BF16),
+            pltpu.SMEM((2, 3), jnp.int32),
+            pltpu.SMEM((2, 3), jnp.int32),
             pltpu.VMEM((2, NY, NX), BF16),
             pltpu.VMEM((2, NY, NX), BF16),
             pltpu.VMEM((DEVICES, BLOCKS, 16, LANES), F32),
@@ -385,23 +420,29 @@
             pltpu.VMEM((2, NZ * 8, LANES), F32),
             pltpu.VMEM((DEVICES, 16, LANES), F32),
         ]
-        + [pltpu.SemaphoreType.DMA] * 10,
+        + [pltpu.SemaphoreType.DMA] * 11
+        + [pltpu.SemaphoreType.DMA((3,)), pltpu.SemaphoreType.DMA((6,))],
         compiler_params=pltpu.CompilerParams(
-            collective_id=0, has_side_effects=True, vmem_limit_bytes=60 << 20
+            collective_id=0, has_side_effects=True, vmem_limit_bytes=46 << 20
         ),
     )(
-        frames[0],
-        jnp.asarray(forward_y_table()),
-        jnp.asarray(forward_x_table()),
-        jnp.asarray(z_table(False)),
-        jnp.asarray(z_table(True)),
-        jnp.asarray(inverse_x_table()),
-        jnp.asarray(inverse_y_table()),
-        shifts,
-        offsets,
-        ref_spectrum.reshape(2, NZ * 8, NX),
+        *(
+            pltpu.with_memory_space_constraint(x, pltpu.HBM)
+            for x in (
+                frames[0],
+                jnp.asarray(forward_y_table()),
+                jnp.asarray(forward_x_table()),
+                jnp.asarray(z_table(False)),
+                jnp.asarray(z_table(True)),
+                jnp.asarray(inverse_x_table()),
+                jnp.asarray(inverse_y_table()),
+                shifts,
+                offsets,
+                ref_spectrum.reshape(2, NZ * 8, NX),
+            )
+        )
     )
-    new = new.reshape(2, BLOCKS, NZ // 2, 8, LANES).transpose(0, 2, 3, 1, 4)
+    new = new.reshape(2, NZ // 2, BLOCKS, 8, LANES).transpose(0, 1, 3, 2, 4)
     return corr[None], new.reshape(2, NZ // 2, 8, NX)
 
 

time: 109 us -> 102 us (0.936); the launches traced: 108 us -> 100 us
  Pallas kernels: 104 us -> 97.7 us
  local copies, waits for them, and re-layouts: 3.9 us -> 1.98 us
    pallas_call x1, Pallas kernels: 104 us -> 97.7 us  [local(): pl.pallas_call(kernel, out_shape=(jax.ShapeDtypeStruct((2, CROP, CROP), F...]
    reshape x1 -> x0, local copies, waits for them, and re-layouts: 3.24 us -> none  [local(): return (corr[None], new.reshape(2, NZ // 2, 8, NX))]
    unnamed x3 -> x2, local copies, waits for them, and re-layouts: 0.66 us -> 1.98 us
where the time goes in v2:
time: 102 us; the launch traced here: 100 us
  Pallas kernels  97.7 us (96%)
  local copies, waits for them, and re-layouts  1.98 us (2%)
    pallas_call x1, Pallas kernels, local(): pl.pallas_call(kernel, out_shape=(jax.ShapeDtypeStruct((2, CROP, CROP), F...  97.7 us

profile of v2, /device:TPU:5, one launch (start us, length us, event | category | flops | bytes accessed | tf_op | source)
XLA Modules:
  0.0 100.3 jit_solution(16758488437104561829)
XLA Ops:
  0.6 97.7 %shard_map.113 = (f32[2,128,128]{2,1,0:T(8,128)S(1)}, f32[2,2048,128]{2,1,0:T(8,128)S(1)}) custom-call(f32[2,512,512]{2,1,0:T(8,128)} %bitcast.11, bf16[2,640,512]{2,1,0:T(8,128)(2,1)} %constant.12.clone.dy_hbm, bf16[2,512,1024]{2,1,0:T(8,128)(2,1)} %constant.13.clone.cs_hbm, bf16[2,256,256]{2,1,0:T(8,128)(2,1)} %constant.14.clone.zf_hbm, ...), custom_call_target="tpu_custom_call" | custom-call | tf_op jit(solution)/shard_map/pallas_call | solution.py:386
  98.3 0.7 copy.14
  99.0 1.3 %copy.15 = f32[2,64,8,512]{3,2,1,0:T(8,128)} copy(f32[2,64,8,512]{3,2,1,0:T(8,128)S(1)} %bitcast.8) | data formatting | bytes 4194304

commit v3 on v2

--- a/solution.py
+++ b/solution.py
@@ -24,6 +24,9 @@
 F32 = jnp.float32
 BF16 = jnp.bfloat16
 MESH = pl.DeviceIdType.MESH
+UNROLL = 8
+EARLY = 2
+PASS = 2
 
 
 def halves(table):
@@ -85,6 +88,17 @@
 
 def dot(a, b):
     return jnp.dot(a, b, preferred_element_type=F32)
+
+
+def each(count, body, step):
+    def several(i, carry):
+        for at in range(step):
+            body(step * i + at)
+        return carry
+
+    lax.fori_loop(0, count // step, several, 0)
+    for k in range(count - count % step, count):
+        body(k)
 
 
 def kernel(
@@ -111,12 +125,14 @@
     for copy in early:
         copy.start()
 
-    def greet(k, carry):
+    def other(k):
         to = (me + 104 + k + jnp.where(k >= 24, 1, 0)) % DEVICES
-        pl.semaphore_signal(barrier, 1, device_id=(to % 2, to // 2), device_id_type=MESH)
-        return carry
-
-    lax.fori_loop(0, DEVICES - 1, greet, 0)
+        return to % 2, to // 2
+
+    def greet(k):
+        pl.semaphore_signal(barrier, 1, device_id=other(k), device_id_type=MESH)
+
+    each(DEVICES - 1, greet, UNROLL)
     for copy in late:
         copy.start()
     for b in range(BLOCKS):
@@ -133,8 +149,6 @@
     sub = lax.broadcasted_iota(jnp.int32, (1, 8, NX), 1)
     sigma = jnp.where(sub < 4, 1.0, -1.0).astype(F32)
     first = (sub % 4) == 0
-
-    pair = BLOCKS // 2
 
     def send(chunk, k, which):
         half = (k + upper) % 2
@@ -143,7 +157,7 @@
         within = 2 * ((core + k // 16) % 2) + (g + k // 8) % 2
         to = 64 * half + 16 * to_z + 4 * to_y + within
         slot = jnp.where(half == 0, GROUPS * chunk + 4 * to_z + within, 79 + GROUPS * chunk - 4 * to_z - within)
-        blocks = slice(which * pair, (which + 1) * pair)
+        blocks = slice(PASS, BLOCKS) if which else slice(0, PASS)
         source, target = sbuf.at[slot, blocks], xbuf.at[g, blocks, pl.ds(16 * d, 16)]
 
         @pl.when(to != me)
@@ -156,8 +170,6 @@
         @pl.when(to == me)
         def _():
             pltpu.make_async_copy(source, target, own_sem).start()
-
-        return 0
 
     def forward(i, carry):
         chunk = (y_at + z_at + i) % CHUNKS
@@ -183,11 +195,11 @@
         def _():
             pl.semaphore_wait(barrier, DEVICES - 1)
 
-        lax.fori_loop(0, 32, lambda k, inner: send(chunk, k, 0), 0)
+        each(32, lambda k: send(chunk, k, 0), 4)
         return carry
 
     lax.fori_loop(0, CHUNKS, forward, 0)
-    lax.fori_loop(0, 32 * CHUNKS, lambda k, inner: send((y_at + z_at + k // 32) % CHUNKS, k % 32, 1), 0)
+    each(32 * CHUNKS, lambda k: send((y_at + z_at + k // 32) % CHUNKS, k % 32, 1), 4)
 
     def row_of(j):
         return jnp.where(upper == 0, j, (4 - j) % 4)
@@ -236,8 +248,8 @@
         return jnp.concatenate(out_re, axis=1), jnp.concatenate(out_im, axis=1)
 
     pltpu.make_async_copy(sbuf.at[0], sbuf.at[0], own_sem).wait()
-    arrivals = sbuf.at[pl.ds(0, DEVICES - 1), 0:pair]
-    pltpu.make_async_copy(arrivals, arrivals, recv_x).wait()
+    ahead, behind = sbuf.at[pl.ds(0, DEVICES - 1), 0:PASS], sbuf.at[pl.ds(0, DEVICES - 1), PASS:BLOCKS]
+    pltpu.make_async_copy(ahead, ahead, recv_x).wait()
 
     half = NZ // 2
 
@@ -248,9 +260,9 @@
         )
 
     def spectrum(b, sums):
-        @pl.when(b == pair)
+        @pl.when(b == PASS)
         def _():
-            pltpu.make_async_copy(arrivals, arrivals, recv_y).wait()
+            pltpu.make_async_copy(behind, behind, recv_y).wait()
 
         zh, zl = zf[0], zf[1]
         ref_re, ref_im = rbuf[0, b], rbuf[1, b]
@@ -276,7 +288,7 @@
         nbuf[b, 0] = new_re
         nbuf[b, 1] = new_im
 
-        @pl.when(b == 0)
+        @pl.when(b < EARLY)
         def _():
             to_partner(b).start()
 
@@ -287,17 +299,15 @@
     lane1 = lax.broadcasted_iota(jnp.int32, (1, LANES), 1)
     mine[...] = jnp.where(lane1 < 64, jnp.sum(sums[0]), jnp.sum(sums[1]))
 
-    def tell(k, carry):
-        to = (me + k) % DEVICES
+    def tell(k):
         pltpu.make_async_remote_copy(
-            mine, abuf.at[me], send_a, recv_a, device_id=(to % 2, to // 2), device_id_type=MESH
+            mine, abuf.at[me], send_a, recv_a, device_id=other(k), device_id_type=MESH
         ).start()
-        return carry
-
-    lax.fori_loop(1, DEVICES, tell, 0)
+
+    each(DEVICES - 1, tell, UNROLL)
     pltpu.make_async_copy(mine, abuf.at[me], own_sem).start()
 
-    for b in range(1, BLOCKS):
+    for b in range(EARLY, BLOCKS):
         to_partner(b).start()
 
     def keep(source, at_grp):
@@ -310,6 +320,13 @@
 
     keep(nbuf.at[:, :, pl.ds(g * half, half)], g)
 
+    def turn(b, carry):
+        for t in range(2):
+            cbuf[t, b, :NZ], cbuf[t, b, NZ:] = turned(1, t, b, cbuf[t, b, :NZ], cbuf[t, b, NZ:])
+        return carry
+
+    lax.fori_loop(0, BLOCKS, turn, 0)
+
     pltpu.make_async_copy(mine, abuf.at[me], own_sem).wait()
     pltpu.make_async_copy(abuf.at[pl.ds(0, DEVICES - 1)], abuf.at[pl.ds(0, DEVICES - 1)], recv_a).wait()
     total = jnp.sum(abuf[...].reshape(DEVICES, LANES), axis=0, keepdims=True) / (NZ * NY * NX)
@@ -321,8 +338,7 @@
         def whiten(b, inner):
             zh, zl = zi[0], zi[1]
             scale = 1.0 / (mbuf[t, b] + average)
-            wr, wi = turned(1, t, b, cbuf[t, b, :NZ] * scale, cbuf[t, b, NZ:] * scale)
-            both = jnp.concatenate([wr, wi], axis=0)
+            both = cbuf[t, b] * jnp.concatenate([scale, scale], axis=0)
             bh, bl = split(both)
             depth = dot(zh, bh) + dot(zl, bh) + dot(zh, bl)
             dh, dl = split(depth)
@@ -343,7 +359,7 @@
                     j * NZ : (j + 1) * NZ, part * CROP : (part + 1) * CROP
                 ]
 
-        def send(k, inner):
+        def send_back(k):
             to = (d + k) % 64
 
             @pl.when((to != d) | (t != g))
@@ -357,12 +373,13 @@
             def _():
                 pltpu.make_async_copy(gbuf.at[t, pl.ds(16 * to, 16)], ybuf.at[me], own_sem).start()
 
-            return inner
-
-        lax.fori_loop(0, 64, send, 0)
+        each(64, send_back, 4)
         return carry
 
     lax.fori_loop(0, 2, back, 0)
+
+    pltpu.make_async_copy(nrecv, nrecv, recv_n).wait()
+    keep(nrecv, 1 - g)
 
     pltpu.make_async_copy(ybuf.at[0], ybuf.at[0], own_sem).wait()
     pltpu.make_async_copy(ybuf.at[pl.ds(0, DEVICES - 1)], ybuf.at[pl.ds(0, DEVICES - 1)], recv_g).wait()
@@ -370,9 +387,6 @@
         rows = ybuf[:, p * 8 : p * 8 + 8, :].reshape(DEVICES * 8, CROP)
         rh, rl = split(rows)
         corr[p] = dot(yi[0], rh) + dot(yi[1], rh) + dot(yi[0], rl)
-
-    pltpu.make_async_copy(nrecv, nrecv, recv_n).wait()
-    keep(nrecv, 1 - g)
 
     pltpu.make_async_copy(sbuf.at[pl.ds(0, DEVICES - 1)], sbuf.at[pl.ds(0, DEVICES - 1)], send_x).wait()
     pltpu.make_async_copy(abuf.at[pl.ds(0, DEVICES - 1)], abuf.at[pl.ds(0, DEVICES - 1)], send_a).wait()

time: 102 us -> 96.4 us (0.945)
  Pallas kernels: 97.7 us -> 92.8 us
    pallas_call x1, Pallas kernels: 97.7 us -> 92.8 us  [local(): pl.pallas_call(kernel, out_shape=(jax.ShapeDtypeStruct((2, CROP, CROP), F...]
where the time goes in v3:
time: 96.4 us; the launch traced here: 95.5 us
  Pallas kernels  92.8 us (96%)
  local copies, waits for them, and re-layouts  1.98 us (2%)
    pallas_call x1, Pallas kernels, local(): pl.pallas_call(kernel, out_shape=(jax.ShapeDtypeStruct((2, CROP, CROP), F...  92.8 us
    unnamed x2, local copies, waits for them, and re-layouts  1.98 us

profile of v3, /device:TPU:5, one launch (start us, length us, event | category | flops | bytes accessed | tf_op | source)
XLA Modules:
  0.0 95.5 jit_solution(11540023068003559503)
XLA Ops:
  0.6 92.8 %shard_map.113 = (f32[2,128,128]{2,1,0:T(8,128)S(1)}, f32[2,2048,128]{2,1,0:T(8,128)S(1)}) custom-call(f32[2,512,512]{2,1,0:T(8,128)} %bitcast.11, bf16[2,640,512]{2,1,0:T(8,128)(2,1)} %constant.12.clone.dy_hbm, bf16[2,512,1024]{2,1,0:T(8,128)(2,1)} %constant.13.clone.cs_hbm, bf16[2,256,256]{2,1,0:T(8,128)(2,1)} %constant.14.clone.zf_hbm, ...), custom_call_target="tpu_custom_call" | custom-call | tf_op jit(solution)/shard_map/pallas_call | solution.py:400
  93.5 0.7 copy.14
  94.1 1.3 %copy.15 = f32[2,64,8,512]{3,2,1,0:T(8,128)} copy(f32[2,64,8,512]{3,2,1,0:T(8,128)S(1)} %bitcast.8) | data formatting | bytes 4194304

commit v4 on v3

--- a/solution.py
+++ b/solution.py
@@ -103,10 +103,10 @@
 
 def kernel(
     frames_hbm, dy_hbm, cs_hbm, zf_hbm, zi_hbm, xi_hbm, yi_hbm, shifts_hbm, offsets_hbm, ref_hbm,
-    corr, nout,
-    frames, dy, cs, zf, zi, xi, yi, shifts, offsets,
+    ybuf, nout, yi,
+    frames, dy, cs, zf, zi, xi, shifts, offsets,
     fhi, flo, sbuf, xbuf, rin, rbuf, cbuf, mbuf, nbuf, nrecv, ramp_xy, ramp_z,
-    mine, abuf, g1hi, g1lo, gbuf, ybuf,
+    mine, abuf, g1hi, g1lo, gbuf,
     send_x, recv_x, send_a, recv_a, send_n, recv_n, send_g, recv_g, ref_sem, own_sem,
     recv_y, first_sem, table_sem,
 ):
@@ -383,28 +383,33 @@
 
     pltpu.make_async_copy(ybuf.at[0], ybuf.at[0], own_sem).wait()
     pltpu.make_async_copy(ybuf.at[pl.ds(0, DEVICES - 1)], ybuf.at[pl.ds(0, DEVICES - 1)], recv_g).wait()
-    for p in range(2):
-        rows = ybuf[:, p * 8 : p * 8 + 8, :].reshape(DEVICES * 8, CROP)
-        rh, rl = split(rows)
-        corr[p] = dot(yi[0], rh) + dot(yi[1], rh) + dot(yi[0], rl)
-
     pltpu.make_async_copy(sbuf.at[pl.ds(0, DEVICES - 1)], sbuf.at[pl.ds(0, DEVICES - 1)], send_x).wait()
     pltpu.make_async_copy(abuf.at[pl.ds(0, DEVICES - 1)], abuf.at[pl.ds(0, DEVICES - 1)], send_a).wait()
     pltpu.make_async_copy(ybuf.at[pl.ds(0, DEVICES - 1)], ybuf.at[pl.ds(0, DEVICES - 1)], send_g).wait()
     pltpu.make_async_copy(nrecv, nrecv, send_n).wait()
 
 
+def finish(ybuf, rows, yi, corr, out, sem):
+    copy = pltpu.make_async_copy(rows, out, sem)
+    copy.start()
+    for p in range(2):
+        high, low = split(ybuf[:, p * 8 : p * 8 + 8, :].reshape(DEVICES * 8, CROP))
+        corr[p] = dot(yi[0], high) + dot(yi[1], high) + dot(yi[0], low)
+    copy.wait()
+
+
 def local(frames, ref_spectrum, shifts, offsets):
     vmem = pl.BlockSpec(memory_space=pltpu.VMEM)
     hbm = pl.BlockSpec(memory_space=pltpu.HBM)
-    corr, new = pl.pallas_call(
+    planes, rows, table = pl.pallas_call(
         kernel,
         out_shape=(
-            jax.ShapeDtypeStruct((2, CROP, CROP), F32),
+            jax.ShapeDtypeStruct((DEVICES, 16, LANES), F32),
             jax.ShapeDtypeStruct((2, NZ // 2 * BLOCKS * 8, LANES), F32),
+            jax.ShapeDtypeStruct((2, CROP, DEVICES * 8), BF16),
         ),
         in_specs=[hbm] * 10,
-        out_specs=(vmem, vmem),
+        out_specs=(vmem, vmem, vmem),
         scratch_shapes=[
             pltpu.VMEM((2, NY, NX), F32),
             pltpu.VMEM((2, CHUNKS * SPAN, NY), BF16),
@@ -412,7 +417,6 @@
             pltpu.VMEM((2, 2 * NZ, 2 * NZ), BF16),
             pltpu.VMEM((2, 2 * NZ, 2 * NZ), BF16),
             pltpu.VMEM((2, 2 * NX, 2 * CROP), BF16),
-            pltpu.VMEM((2, CROP, DEVICES * 8), BF16),
             pltpu.SMEM((2, 3), jnp.int32),
             pltpu.SMEM((2, 3), jnp.int32),
             pltpu.VMEM((2, NY, NX), BF16),
@@ -432,7 +436,6 @@
             pltpu.VMEM((ROWS * NZ, 2 * NX), BF16),
             pltpu.VMEM((ROWS * NZ, 2 * NX), BF16),
             pltpu.VMEM((2, NZ * 8, LANES), F32),
-            pltpu.VMEM((DEVICES, 16, LANES), F32),
         ]
         + [pltpu.SemaphoreType.DMA] * 11
         + [pltpu.SemaphoreType.DMA((3,)), pltpu.SemaphoreType.DMA((6,))],
@@ -456,6 +459,17 @@
             )
         )
     )
+    corr, new = pl.pallas_call(
+        finish,
+        out_shape=(
+            jax.ShapeDtypeStruct((2, CROP, CROP), F32),
+            jax.ShapeDtypeStruct(rows.shape, F32),
+        ),
+        in_specs=[vmem] * 3,
+        out_specs=(vmem, hbm),
+        scratch_shapes=[pltpu.SemaphoreType.DMA],
+        compiler_params=pltpu.CompilerParams(vmem_limit_bytes=16 << 20),
+    )(planes, rows, table)
     new = new.reshape(2, NZ // 2, BLOCKS, 8, LANES).transpose(0, 1, 3, 2, 4)
     return corr[None], new.reshape(2, NZ // 2, 8, NX)
 

time: 96.4 us -> 95.9 us (level)
  local copies, waits for them, and re-layouts: 1.98 us -> 0 us
  Pallas kernels: 92.8 us -> 94.3 us
    unnamed x2 -> x0, local copies, waits for them, and re-layouts: 1.98 us -> none
    pallas_call x1 -> x2, Pallas kernels: 92.8 us -> 94.3 us  [the longest x1 92.3 us: local(): pl.pallas_call(kernel, out_shape=(jax.ShapeDtypeStruct((DEVICES, 16, LANE...]
where the time goes in v4:
time: 95.9 us; the launch traced here: 95 us
  Pallas kernels  94.3 us (98%)
    pallas_call x1, Pallas kernels, local(): pl.pallas_call(kernel, out_shape=(jax.ShapeDtypeStruct((DEVICES, 16, LANE...  92.3 us
    pallas_call x1, Pallas kernels, local(): pl.pallas_call(finish, out_shape=(jax.ShapeDtypeStruct((2, CROP, CROP), F...  2.04 us

profile of v4, /device:TPU:5, one launch (start us, length us, event | category | flops | bytes accessed | tf_op | source)
XLA Modules:
  0.0 95.0 jit_solution(14607281486256946823)
XLA Ops:
  0.6 92.3 %shard_map.113 = (f32[128,16,128]{2,1,0:T(8,128)S(1)}, f32[2,2048,128]{2,1,0:T(8,128)S(1)}, bf16[2,128,1024]{2,1,0:T(8,128)(2,1)S(1)}) custom-call(f32[2,512,512]{2,1,0:T(8,128)} %bitcast.9, bf16[2,640,512]{2,1,0:T(8,128)(2,1)} %constant.12.clone.dy_hbm, bf16[2,512,1024]{2,1,0:T(8,128)(2,1)} %constant.13.clone.cs_hbm, ...), custom_call_target="tpu_custom_call" | custom-call | tf_op jit(solution)/shard_map/pallas_call | solution.py:404
  92.9 2.0 %shard_map.114 = (f32[2,128,128]{2,1,0:T(8,128)}, f32[2,2048,128]{2,1,0:T(8,128)}) custom-call(f32[128,16,128]{2,1,0:T(8,128)S(1)} %get-tuple-element.7.ybuf, f32[2,2048,128]{2,1,0:T(8,128)S(1)} %get-tuple-element.8.rows, bf16[2,128,1024]{2,1,0:T(8,128)(2,1)S(1)} %get-tuple-element.9.yi), custom_call_target="tpu_custom_call" | custom-call | tf_op jit(solution)/shard_map/pallas_call | solution.py:462

commit v5 on v4

--- a/solution.py
+++ b/solution.py
@@ -132,7 +132,7 @@
     def greet(k):
         pl.semaphore_signal(barrier, 1, device_id=other(k), device_id_type=MESH)
 
-    each(DEVICES - 1, greet, UNROLL)
+    each(DEVICES - 1, greet, 16)
     for copy in late:
         copy.start()
     for b in range(BLOCKS):
@@ -392,9 +392,11 @@
 def finish(ybuf, rows, yi, corr, out, sem):
     copy = pltpu.make_async_copy(rows, out, sem)
     copy.start()
+    planes = [ybuf[:, p * 8 : p * 8 + 8, :].reshape(DEVICES * 8, CROP) for p in range(2)]
+    high, low = split(jnp.concatenate(planes, axis=1))
+    both = dot(yi[0], high) + dot(yi[1], high) + dot(yi[0], low)
     for p in range(2):
-        high, low = split(ybuf[:, p * 8 : p * 8 + 8, :].reshape(DEVICES * 8, CROP))
-        corr[p] = dot(yi[0], high) + dot(yi[1], high) + dot(yi[0], low)
+        corr[p] = both[:, p * CROP : (p + 1) * CROP]
     copy.wait()
 
 

time: 95.9 us -> 95.9 us (level)
  no operation moved by 1% of the time
where the time goes in v5:
time: 95.9 us; the launch traced here: 94.7 us
  Pallas kernels  94.1 us (98%)
    pallas_call x1, Pallas kernels, local(): pl.pallas_call(kernel, out_shape=(jax.ShapeDtypeStruct((DEVICES, 16, LANE...  92 us
    pallas_call x1, Pallas kernels, local(): pl.pallas_call(finish, out_shape=(jax.ShapeDtypeStruct((2, CROP, CROP), F...  2.07 us

profile of v5, /device:TPU:5, one launch (start us, length us, event | category | flops | bytes accessed | tf_op | source)
XLA Modules:
  0.0 94.7 jit_solution(13806502605683903710)
XLA Ops:
  0.6 92.0 %shard_map.113 = (f32[128,16,128]{2,1,0:T(8,128)S(1)}, f32[2,2048,128]{2,1,0:T(8,128)S(1)}, bf16[2,128,1024]{2,1,0:T(8,128)(2,1)S(1)}) custom-call(f32[2,512,512]{2,1,0:T(8,128)} %bitcast.9, bf16[2,640,512]{2,1,0:T(8,128)(2,1)} %constant.12.clone.dy_hbm, bf16[2,512,1024]{2,1,0:T(8,128)(2,1)} %constant.13.clone.cs_hbm, ...), custom_call_target="tpu_custom_call" | custom-call | tf_op jit(solution)/shard_map/pallas_call | solution.py:406
  92.6 2.1 %shard_map.114 = (f32[2,128,128]{2,1,0:T(8,128)}, f32[2,2048,128]{2,1,0:T(8,128)}) custom-call(f32[128,16,128]{2,1,0:T(8,128)S(1)} %get-tuple-element.7.ybuf, f32[2,2048,128]{2,1,0:T(8,128)S(1)} %get-tuple-element.8.rows, bf16[2,128,1024]{2,1,0:T(8,128)(2,1)S(1)} %get-tuple-element.9.yi), custom_call_target="tpu_custom_call" | custom-call | tf_op jit(solution)/shard_map/pallas_call | solution.py:464
